TPU v7x, 128 devices: a 2x2x16 block of a 8x8x16 slice. The times are simulated.
128 devices in a mesh: grp: 4 (over y, x), seq: 32 (over z, core).
Axes of the slice: x: 2, y: 2, z: 16, core: 2. Of those that a mesh axis runs over, the one named last changes fastest.
The devices are a block of a 8x8x16 slice.
Arguments:
- queries: bfloat16 [2048, 4096], P(('grp', 'seq')), parts along dimension 0, may hold values from -36 to 36
- new_keys: bfloat16 [2048, 1024], P(('grp', 'seq')), parts along dimension 0, may hold values from -24 to 24
- new_values: bfloat16 [2048, 1024], P(('grp', 'seq')), parts along dimension 0, may hold values from -12 to 12
- suffix_keys: bfloat16 [2048, 256, 1024], P(('grp', 'seq')), parts along dimension 0, may hold values from -18 to 18
- suffix_values: bfloat16 [2048, 256, 1024], P(('grp', 'seq')), parts along dimension 0, may hold values from -12 to 12
- suffix_lens: int32 [2048], P(('grp', 'seq')), parts along dimension 0, may hold values from 1 to 256, 65536 in all
- prefix_keys: bfloat16 [8192, 16, 1024], P(('grp', 'seq')), parts along dimension 0, may hold values from -12 to 12
- prefix_values: bfloat16 [8192, 16, 1024], P(('grp', 'seq')), parts along dimension 0, may hold values from -12 to 12
- page_table: int32 [8, 1024], P('grp'), parts along dimension 0, may hold values from 0 to 2047, as said below
- prefix_id: int32 [2048], P('grp'), parts along dimension 0, may hold values from 0 to 1
Outputs:
- attn_out: bfloat16 [2048, 4096], P(('grp', 'seq')), parts along dimension 0
There are 4 independent parts, one for each index of `grp`. A program takes and returns all parts, laid end to end along the dimension named above; each array names one. Nothing has to cross between parts.
Inputs may be any that keep to these rules, and one draw needn't show every extreme that they name: `page_table`: every page id 0 to 2047 stands exactly once in the table. Each run of 64 page ids that starts at a multiple of 64 holds at least one page of every prefix.
All inputs are finite; a program needn't handle non-finite values. No bound on the sum of `suffix_lens` on one device may be relied on, other than what follows from the above.
Results may differ from a plain program's by a relative error of at most 0.005.
Values may be sent and summed in bfloat16 or wider, within the bound.
No kernel may reach another device: no remote copies, remote signals or barrier semaphores. Data moves between devices by JAX's collectives and lax.ppermute only.
A program may use at most 192 MiB of HBM per device.

v0:
```python
import math
import jax
import jax.numpy as jnp
from jax import lax
from jax.sharding import Mesh
from jax.sharding import PartitionSpec as P

H = 32
KV = 8
HD = 128
NPREF = 2
SEQ = ("seq_0", "seq_1")
GRP_SEQ = ("grp", "seq_0", "seq_1")
floor_score = -1e30


def split_up(array, dim, peers):
    before, after = (array.shape[:dim], array.shape[dim + 1 :])
    return jnp.moveaxis(array.reshape(*before, peers, -1, *after), dim, 0)


def laid_out(tiles, dim):
    tiles = jnp.moveaxis(tiles, 0, dim)
    lengths = tiles.shape
    return tiles.reshape(*lengths[:dim], lengths[dim] * lengths[dim + 1], *lengths[dim + 2 :])


def moved_by_axis(tiles, axes, sequence):
    lengths = [lax.axis_size(a) for a in axes]
    tiles = tiles.reshape(*lengths, *tiles.shape[1:])
    for k in sequence:
        tiles = lax.all_to_all(tiles, axes[k], split_axis=k, concat_axis=k, tiled=True)
    return tiles.reshape(-1, *tiles.shape[len(axes) :])


def two_step_exchange(array, groups, sequence, split_dim, concat_dim):
    peers = lax.axis_size(groups[0]) * lax.axis_size(groups[1])
    tiles = split_up(array, split_dim, peers)
    return laid_out(moved_by_axis(tiles, groups, sequence), concat_dim)


def local(
    queries,
    new_keys,
    new_values,
    suffix_keys,
    suffix_values,
    suffix_lens,
    prefix_keys,
    prefix_values,
    page_table,
    prefix_id,
):
    local_rows = queries.shape[0]
    group_size = H // KV
    softmax_scale = 1.0 / math.sqrt(HD)
    owner_count = lax.axis_size(SEQ)
    owner_index = lax.axis_index(SEQ)
    pages_dev = prefix_keys.shape[0]
    local_ids = owner_index * pages_dev + jnp.arange(pages_dev, dtype=jnp.int32)
    page_hits = jnp.any(page_table[:, :, None] == local_ids[None, None, :], axis=1)
    page_label = jnp.sum(
        page_hits.astype(jnp.int32) * jnp.arange(NPREF, dtype=jnp.int32)[:, None], axis=0
    )
    token_label = jnp.repeat(page_label, prefix_keys.shape[1])
    keys_local = prefix_keys.reshape(-1, KV, HD)
    values_local = prefix_values.reshape(-1, KV, HD)
    shard_rows = lax.all_gather(queries, SEQ, axis=0, tiled=True)
    piece_rows = shard_rows.shape[0]
    query_head_count = shard_rows.reshape(piece_rows, KV, group_size, HD)
    scores = (
        jnp.einsum(
            "bkgd,tkd->bkgt", query_head_count, keys_local, preferred_element_type=jnp.float32
        )
        * softmax_scale
    )
    allowed = (prefix_id[:, None] == token_label[None, :])[:, None, None, :]
    scores = jnp.where(allowed, scores, floor_score)
    row_peak = jnp.max(scores, axis=3)
    weights = jnp.where(allowed, jnp.exp(scores - row_peak[..., None]), 0.0)
    weight_sum = jnp.sum(weights, axis=3)
    numerator = jnp.einsum(
        "bkgt,tkd->bkgd",
        weights.astype(jnp.bfloat16),
        values_local,
        preferred_element_type=jnp.float32,
    )
    piece_out = (numerator / weight_sum[..., None]).astype(jnp.bfloat16).reshape(piece_rows, -1)
    piece_lse = (row_peak + jnp.log(weight_sum)).reshape(-1)
    out_all = piece_out
    lse_all = piece_lse
    out_all, lse_all = (out_all, lse_all)
    resident_heads = queries.reshape(local_rows, KV, group_size, HD)
    slot_count = suffix_keys.shape[1]
    own_keys = suffix_keys.reshape(local_rows, slot_count, KV, HD)
    own_values = suffix_values.reshape(local_rows, slot_count, KV, HD)
    suffix_scores = (
        jnp.einsum("bkgd,btkd->bkgt", resident_heads, own_keys, preferred_element_type=jnp.float32)
        * softmax_scale
    )
    suffix_live = (jnp.arange(slot_count, dtype=jnp.int32)[None, :] < suffix_lens[:, None])[
        :, None, None, :
    ]
    suffix_scores = jnp.where(suffix_live, suffix_scores, floor_score)
    incoming_keys = new_keys.reshape(local_rows, KV, HD)
    incoming_values = new_values.reshape(local_rows, KV, HD)
    incoming_scores = (
        jnp.einsum(
            "iqnc,iqc->iqn", resident_heads, incoming_keys, preferred_element_type=jnp.float32
        )
        * softmax_scale
    )
    home_peak = jnp.maximum(jnp.max(suffix_scores, axis=3), incoming_scores)
    suffix_weights = jnp.where(suffix_live, jnp.exp(suffix_scores - home_peak[..., None]), 0.0)
    fresh_weights = jnp.exp(incoming_scores - home_peak)
    home_mass = jnp.sum(suffix_weights, axis=3) + fresh_weights
    resident_numerator = jnp.einsum(
        "bkgt,btkd->bkgd",
        suffix_weights.astype(jnp.bfloat16),
        own_values,
        preferred_element_type=jnp.float32,
    )
    resident_numerator = resident_numerator + jnp.einsum(
        "cqx,cqh->cqxh",
        fresh_weights.astype(jnp.bfloat16),
        incoming_values,
        preferred_element_type=jnp.float32,
    )
    home_out = (
        resident_numerator.reshape(local_rows, H, HD) / home_mass.reshape(local_rows, H)[..., None]
    )
    home_lse = (home_peak + jnp.log(home_mass)).reshape(local_rows, H)
    recv_out = lax.all_to_all(out_all, SEQ, split_axis=0, concat_axis=0, tiled=True)
    recv_lse = two_step_exchange(lse_all, ("seq_0", "seq_1"), (0, 1), 0, 0)
    recv_out = recv_out.reshape(owner_count, local_rows, H, HD).astype(jnp.float32)
    recv_lse = recv_lse.reshape(owner_count, local_rows, H)
    overall = jnp.maximum(jnp.max(recv_lse, axis=0), home_lse)
    factor = jnp.exp(recv_lse - overall[None])
    home_factor = jnp.exp(home_lse - overall)
    merged = jnp.sum(factor[..., None] * recv_out, axis=0) + home_factor[..., None] * home_out
    divisor = jnp.sum(factor, axis=0) + home_factor
    result = merged / divisor[..., None]
    return result.reshape(local_rows, H * HD).astype(jnp.bfloat16)


def solution(mesh):
    finer = Mesh(mesh.devices.reshape(mesh.shape["grp"], 16, 2), ("grp", "seq_0", "seq_1"))
    placed = (
        P(GRP_SEQ, None),
        P(GRP_SEQ, None),
        P(GRP_SEQ, None),
        P(GRP_SEQ, None, None),
        P(GRP_SEQ, None, None),
        P(GRP_SEQ),
        P(GRP_SEQ, None, None),
        P(GRP_SEQ, None, None),
        P("grp", None),
        P("grp"),
    )
    return jax.shard_map(
        local, mesh=finer, in_specs=placed, out_specs=P(GRP_SEQ, None), check_vma=False
    )
```

profile of v0, /device:TPU:196, one launch (start us, length us, event | category | flops | bytes accessed | tf_op | source)
XLA Modules:
  0.0 416.6 jit_solution(18046694975865880735)
XLA Ops:
  6.5 0.0 all-gather.2.cloned.1.call-start
  6.6 0.7 all-gather.2.cloned.1.call-update
  7.3 0.9 compare_reduce_fusion
  8.3 0.1 broadcast_in_dim.54
  8.3 0.1 eq.36
  8.4 2.2 copy.106
  10.6 3.6 copy.107
  14.2 0.0 copy-done.3
  14.2 0.4 broadcast_compare_fusion
  14.6 70.5 %all-gather.2.cloned.1.call-done = bf16[512,4096]{1,0:T(8,128)(2,1)} async-done(((bf16[16,4096]{1,0:T(8,128)(2,1)}), bf16[512,4096]{1,0:T(8,128)(2,1)}) %all-gather.2.cloned.1.call-update) | async-done | bytes 4194320 | tf_op jit(solution)/shard_map/all_gather | solution.py:68
  85.1 6.5 %copy.78 = bf16[512,4096]{0,1:T(8,128)(2,1)} copy(bf16[512,4096]{1,0:T(8,128)(2,1)} %all-gather.2.cloned.1.call-done) | data formatting | bytes 8388608 | tf_op jit(solution)/shard_map/all_gather | solution.py:68
  91.6 27.0 %fusion = (f32[512,8,4]{0,2,1:T(4,128)S(1)}, f32[8,1024,512,4]{2,1,3,0:T(8,128)}) fusion(pred[512,1024]{0,1:T(8,128)(4,1)S(1)} %broadcast_compare_fusion, bf16[512,8,4,128]{0,3,2,1:T(8,128)(2,1)} %bitcast.83, bf16[1024,8,128,1]{2,1,0,3:T(8,128)(2,1)S(1)} %bitcast.84), kind=kOutput, calls=%fused_computation.2 | convolution fusion | flops 4345282560 | bytes 73990144 | tf_op jit(solution)/shard_map/bkgd,tkd->bkgt/dot_general | solution.py:72
  118.6 21.8 %fusion.2 = f32[512,8,4]{0,2,1:T(4,128)S(1)} fusion(f32[8,1024,512,4]{2,1,3,0:T(8,128)} %get-tuple-element.13, f32[512,8,4]{0,2,1:T(4,128)S(1)} %get-tuple-element.12, pred[512,1024]{0,1:T(8,128)(4,1)S(1)} %broadcast_compare_fusion), kind=kLoop, calls=%fused_computation.4 | loop fusion | flops 83869696 | bytes 67764224 | tf_op jit(solution)/shard_map/reduce_sum | solution.py:81
  140.4 0.8 copy.81
  141.2 2.3 add.44
  143.5 8.4 %all-to-all-start = ((f32[16,2,512]{2,1,0:T(2,128)}), f32[16,2,512]{2,1,0:T(2,128)S(1)}, u32[]{:S(2)}, u32[]{:S(2)}) async-start(f32[16,2,512]{2,1,0:T(2,128)} %add.44), calls=%async_computation | async-start | bytes 131072 | tf_op jit(solution)/shard_map/all_to_all | solution.py:32
  151.9 29.9 %fusion.12 = bf16[512,8,4,128]{3,0,2,1:T(8,128)(2,1)} fusion(f32[512,8,4]{0,2,1:T(4,128)S(1)} %fusion.2, f32[8,1024,512,4]{2,1,3,0:T(8,128)} %get-tuple-element.13, f32[512,8,4]{0,2,1:T(4,128)S(1)} %get-tuple-element.12, pred[512,1024]{0,1:T(8,128)(4,1)S(1)} %broadcast_compare_fusion, bf16[1024,8,128,1]{2,1,0,3:T(8,128)(2,1)} %bitcast.87), kind=kOutput, calls=%fused_computation.14 | convolution fusion | flops 4383047680 | bytes 74055680 | tf_op jit(solution)/shard_map/bkgt,tkd->bkgd/dot_general | solution.py:82
  181.8 7.3 %copy.89 = bf16[512,8,4,128]{3,2,1,0:T(4,128)(2,1)} copy(bf16[512,8,4,128]{3,0,2,1:T(8,128)(2,1)} %fusion.12) | data formatting | bytes 8388608 | tf_op jit(solution)/shard_map/convert_element_type | solution.py:88
  189.2 7.8 %all_to_all.14 = bf16[32,16,4096]{2,1,0:T(8,128)(2,1)} reshape(bf16[512,8,4,128]{3,2,1,0:T(4,128)(2,1)} %copy.89) | data formatting | bytes 8388608 | tf_op jit(solution)/shard_map/all_to_all | solution.py:133
  197.0 0.0 all-to-all-done
  197.1 3.8 all_to_all.19
  200.9 12.6 %all-to-all-start.2 = ((bf16[32,16,4096]{2,1,0:T(8,128)(2,1)}), bf16[32,16,4096]{2,1,0:T(8,128)(2,1)}, u32[]{:S(2)}, u32[]{:S(2)}) async-start(bf16[32,16,4096]{2,1,0:T(8,128)(2,1)} %all_to_all.14), calls=%async_computation.2 | async-start | bytes 8388608 | tf_op jit(solution)/shard_map/all_to_all | solution.py:133
  213.4 0.1 reshape.158
  213.6 0.0 copy-done.4
  213.6 0.1 iota_compare_fusion
  213.7 0.3 fusion.44
  213.9 5.7 %fusion.43 = (f32[16,8,4]{2,1,0:T(8,128)S(1)}, f32[16,8,4,256]{3,2,1,0:T(4,128)S(1)}) fusion(bf16[16,8,4,128]{3,2,1,0:T(4,128)(2,1)S(1)} %reshape.158, pred[16,256]{1,0:T(8,128)(4,1)S(1)} %iota_compare_fusion, bf16[16,256,1024]{2,1,0:T(8,128)(2,1)} %param.13), kind=kOutput, calls=%fused_computation.53 | convolution fusion | flops 33947136 | bytes 9050112 | tf_op jit(solution)/shard_map/bkgd,btkd->bkgt/dot_general | solution.py:98
  219.7 0.4 fusion.28
  220.2 0.1 reshape.166
  220.3 0.1 copy.85
  220.4 0.0 copy-done.2
  220.5 0.1 copy.92
  220.6 0.1 copy.93
  220.7 4.7 %fusion.21 = f32[16,8,4,128]{3,2,1,0:T(4,128)S(1)} fusion(f32[16,8,4,256]{3,2,1,0:T(4,128)S(1)} %get-tuple-element.15, f32[16,8,4]{2,1,0:T(8,128)S(1)} %get-tuple-element.6, pred[16,256]{1,0:T(8,128)(4,1)S(1)} %iota_compare_fusion, f32[16,8,128]{2,1,0:T(8,128)S(1)} %bitcast.98, f32[16,8,4]{2,1,0:T(8,128)S(1)} %get-tuple-element.5, ...), kind=kOutput, calls=%fused_computation.20 | convolution fusion | flops 34078720 | bytes 9248768 | tf_op jit(solution)/shard_map/bkgt,btkd->bkgd/dot_general | solution.py:117
  225.3 0.1 reshape.165
  225.4 0.1 copy.86
  225.5 0.1 reduce_max.31
  225.6 0.1 reduce_sum.52
  225.7 0.1 copy.83
  225.8 0.1 reshape_reshape_reshape.4
  226.0 4.6 %mul.68 = f32[32,16,32,128]{3,2,1,0:T(8,128)} broadcast(f32[32,16,32]{2,1,0:T(8,128)S(1)} %subtract_exponential_fusion), dimensions={0,1,2} | broadcast | bytes 8454144 | tf_op jit(solution)/shard_map/mul | solution.py:140
  230.6 9.4 %mul.69 = f32[32,16,4096]{2,1,0:T(8,128)} reshape(f32[32,16,32,128]{3,2,1,0:T(8,128)} %mul.68) | data formatting | bytes 16777216 | tf_op jit(solution)/shard_map/mul | solution.py:140
  240.0 162.5 %all-to-all-done.2 = bf16[32,16,4096]{2,1,0:T(8,128)(2,1)} async-done(((bf16[32,16,4096]{2,1,0:T(8,128)(2,1)}), bf16[32,16,4096]{2,1,0:T(8,128)(2,1)}, u32[]{:S(2)}, u32[]{:S(2)}) %all-to-all-start.2) | async-done | bytes 4194336 | tf_op jit(solution)/shard_map/all_to_all | solution.py:133
  402.5 5.7 %multiply_reduce_fusion = f32[16,4096]{1,0:T(8,128)S(1)} fusion(f32[32,16,4096]{2,1,0:T(8,128)} %mul.69, bf16[32,16,4096]{2,1,0:T(8,128)(2,1)} %all-to-all-done.2), kind=kLoop, calls=%fused_computation.15 | loop fusion | flops 6225920 | bytes 12845056 | tf_op jit(solution)/shard_map/reduce_sum | solution.py:140
  408.2 0.1 div.35
  408.3 0.1 div.38
  408.5 0.1 mul.71
  408.6 1.1 fusion.30
  (21 shorter events, 0.3 us)
Async XLA Ops:
  6.5 7.7 %copy-start.3 = (s32[512]{0:T(512)S(1)}, s32[512]{0:T(512)}, u32[]{:S(2)}) copy-start(s32[512]{0:T(512)} %param.19) | copy-start | bytes 6148
  6.5 78.6 %all-gather.2.cloned.1.call-start = ((), (), s32[]{:S(2)}) async-start(), calls=%async_computation.3 | async-start | bytes 4325376 | tf_op jit(solution)/shard_map/all_gather | solution.py:68
  143.5 53.5 %all-to-all-start = ((f32[16,2,512]{2,1,0:T(2,128)}), f32[16,2,512]{2,1,0:T(2,128)S(1)}, u32[]{:S(2)}, u32[]{:S(2)}) async-start(f32[16,2,512]{2,1,0:T(2,128)} %add.44), calls=%async_computation | async-start | bytes 131072 | tf_op jit(solution)/shard_map/all_to_all | solution.py:32
  189.2 24.3 %copy-start = (bf16[16,4096]{1,0:T(8,128)(2,1)S(1)}, bf16[16,4096]{1,0:T(8,128)(2,1)}, u32[]{:S(2)}) copy-start(bf16[16,4096]{1,0:T(8,128)(2,1)} %param.10) | copy-start | bytes 393220
  189.2 24.3 %copy-start.1 = (bf16[16,1024]{1,0:T(8,128)(2,1)S(1)}, bf16[16,1024]{1,0:T(8,128)(2,1)}, u32[]{:S(2)}) copy-start(bf16[16,1024]{1,0:T(8,128)(2,1)} %param.11) | copy-start | bytes 98308
  189.2 24.4 %copy-start.4 = (s32[16]{0:T(128)S(1)}, s32[16]{0:T(128)}, u32[]{:S(2)}) copy-start(s32[16]{0:T(128)} %param.15) | copy-start | bytes 196
  200.9 19.6 %copy-start.2 = (bf16[16,1024]{1,0:T(8,128)(2,1)S(1)}, bf16[16,1024]{1,0:T(8,128)(2,1)}, u32[]{:S(2)}) copy-start(bf16[16,1024]{1,0:T(8,128)(2,1)} %param.12) | copy-start | bytes 98308
  200.9 201.7 %all-to-all-start.2 = ((bf16[32,16,4096]{2,1,0:T(8,128)(2,1)}), bf16[32,16,4096]{2,1,0:T(8,128)(2,1)}, u32[]{:S(2)}, u32[]{:S(2)}) async-start(bf16[32,16,4096]{2,1,0:T(8,128)(2,1)} %all_to_all.14), calls=%async_computation.2 | async-start | bytes 8388608 | tf_op jit(solution)/shard_map/all_to_all | solution.py:133
Sparse Core Ops, SparseCore 0:
  9.1 76.0 all-gather.1
where the time goes:
time: 418 us; the launch traced here: 417 us
  waiting for transfers between devices  234 us (56%)
  matrix products  67.5 us (16%)
  local copies, waits for them, and re-layouts  46.3 us (11%)
  other arithmetic  30.6 us (7%)
  starting transfers between devices  21 us (5%)
  between operations  13.7 us (3%)
    all_to_all x1, waiting for transfers between devices, local(): lax.all_to_all(out_all, SEQ, split_axis=0, concat_axis=0, tiled=True)  163 us
    all_gather x1, waiting for transfers between devices, local(): shard_rows = lax.all_gather(queries, SEQ, axis=0, tiled=True)  70.5 us
    dot_general x1, matrix products, local(): jnp.einsum('bkgt,tkd->bkgd', weights.astype(jnp.bfloat16), values_local,...  29.9 us
    dot_general x1, matrix products, local(): jnp.einsum('bkgd,tkd->bkgt', query_head_count, keys_local, preferred_elem...  27 us
    reduce_sum x1, other arithmetic, local(): weight_sum = jnp.sum(weights, axis=3)  21.8 us
    mul x2, local copies, waits for them, and re-layouts, local(): factor[..., None] * recv_out  14 us
    all_to_all x1, starting transfers between devices, local(): lax.all_to_all(out_all, SEQ, split_axis=0, concat_axis=0, tiled=True)  12.6 us
    all_to_all x1, starting transfers between devices, moved_by_axis(): lax.all_to_all(tiles, axes[k], split_axis=k, concat_axis=k, tiled=True)  8.39 us
  transfers between devices with their start and end apart: 3, of which 2 were waited for; matrix products, arithmetic and copies ran while one was open for 17% of the time, Pallas kernels for 0%

commit v1 on v0

--- a/solution.py
+++ b/solution.py
@@ -65,7 +65,9 @@
     token_label = jnp.repeat(page_label, prefix_keys.shape[1])
     keys_local = prefix_keys.reshape(-1, KV, HD)
     values_local = prefix_values.reshape(-1, KV, HD)
-    shard_rows = lax.all_gather(queries, SEQ, axis=0, tiled=True)
+    shard_rows = jnp.concatenate(
+        lax.all_to_all(jnp.stack([queries] * lax.axis_size(SEQ)), SEQ, 0, 0), axis=0
+    )
     piece_rows = shard_rows.shape[0]
     query_head_count = shard_rows.reshape(piece_rows, KV, group_size, HD)
     scores = (

time: 418 us -> 538 us (1.29)
  waiting for transfers between devices: 234 us -> 345 us
  between operations: 13.7 us -> 0.25 us
  starting transfers between devices: 21 us -> 34.3 us
  matrix products: 67.5 us -> 73 us
    all_to_all x0 -> x1, waiting for transfers between devices: none -> 182 us  [local(): lax.all_to_all(jnp.stack([queries] * lax.axis_size(SEQ)), SEQ, 0, 0)]
    all_gather x1 -> x0, waiting for transfers between devices: 70.5 us -> none  [local(): shard_rows = lax.all_gather(queries, SEQ, axis=0, tiled=True)]
    all_to_all x0 -> x1, starting transfers between devices: none -> 17.1 us  [local(): lax.all_to_all(jnp.stack([queries] * lax.axis_size(SEQ)), SEQ, 0, 0)]
    another operation x0 -> x2, local copies, waits for them, and re-layouts: none -> 11.2 us  [the longest x1 7.71 us: local(): query_head_count = shard_rows.reshape(piece_rows, KV, group_size, HD)]
    all_gather x1 -> x0, local copies, waits for them, and re-layouts: 6.54 us -> none  [local(): shard_rows = lax.all_gather(queries, SEQ, axis=0, tiled=True)]
    dot_general x1, matrix products: 27 us -> 32.4 us  [local(): jnp.einsum('bkgd,tkd->bkgt', query_head_count, keys_local, preferred_elem...]
  transfers between devices with their start and end apart: 3 -> 3, of which waited for: 2 -> 2; matrix products, arithmetic and copies ran while one was open for 17% -> 13% of each run, Pallas kernels for 0% -> 0%
where the time goes in v1:
time: 538 us; the launch traced here: 537 us
  waiting for transfers between devices  345 us (64%)
  matrix products  73 us (14%)
  local copies, waits for them, and re-layouts  50.9 us (9%)
  starting transfers between devices  34.3 us (6%)
  other arithmetic  30.1 us (6%)
    all_to_all x1, waiting for transfers between devices, local(): lax.all_to_all(jnp.stack([queries] * lax.axis_size(SEQ)), SEQ, 0, 0)  182 us
    all_to_all x1, waiting for transfers between devices, local(): lax.all_to_all(out_all, SEQ, split_axis=0, concat_axis=0, tiled=True)  163 us
    dot_general x1, matrix products, local(): jnp.einsum('bkgd,tkd->bkgt', query_head_count, keys_local, preferred_elem...  32.4 us
    dot_general x1, matrix products, local(): jnp.einsum('bkgt,tkd->bkgd', weights.astype(jnp.bfloat16), values_local,...  29.9 us
    reduce_sum x1, other arithmetic, local(): weight_sum = jnp.sum(weights, axis=3)  21.9 us
    all_to_all x1, starting transfers between devices, local(): lax.all_to_all(jnp.stack([queries] * lax.axis_size(SEQ)), SEQ, 0, 0)  17.1 us
    mul x2, local copies, waits for them, and re-layouts, local(): factor[..., None] * recv_out  14 us
    all_to_all x1, starting transfers between devices, local(): lax.all_to_all(out_all, SEQ, split_axis=0, concat_axis=0, tiled=True)  12.6 us
  transfers between devices with their start and end apart: 3, of which 2 were waited for; matrix products, arithmetic and copies ran while one was open for 13% of the time, Pallas kernels for 0%

profile of v1, /device:TPU:196, one launch (start us, length us, event | category | flops | bytes accessed | tf_op | source)
XLA Modules:
  0.0 537.3 jit_solution(11735924267567269058)
XLA Ops:
  0.0 3.5 stack.2
  3.5 17.1 %all-to-all-start = ((bf16[32,16,4096]{2,1,0:T(8,128)(2,1)}), bf16[32,16,4096]{2,1,0:T(8,128)(2,1)}, u32[]{:S(2)}, u32[]{:S(2)}) async-start(bf16[32,16,4096]{2,1,0:T(8,128)(2,1)} %stack.2), calls=%async_computation | async-start | bytes 8388608 | tf_op jit(solution)/shard_map/all_to_all | solution.py:69
  20.7 0.0 copy-done.5
  20.7 0.2 compare_reduce_fusion
  21.0 0.1 broadcast_in_dim.54
  21.0 0.1 eq.36
  21.1 0.0 copy-done
  21.1 2.0 copy.100
  23.1 3.7 copy.101
  26.9 0.4 broadcast_compare_fusion
  27.2 182.4 %all-to-all-done = bf16[32,16,4096]{2,1,0:T(8,128)(2,1)} async-done(((bf16[32,16,4096]{2,1,0:T(8,128)(2,1)}), bf16[32,16,4096]{2,1,0:T(8,128)(2,1)}, u32[]{:S(2)}, u32[]{:S(2)}) %all-to-all-start) | async-done | bytes 4194336 | tf_op jit(solution)/shard_map/all_to_all | solution.py:69
  209.6 7.7 %reshape_reshape.3 = bf16[512,8,4,128]{3,2,1,0:T(4,128)(2,1)} reshape(bf16[32,16,4096]{2,1,0:T(8,128)(2,1)} %all-to-all-done) | data formatting | bytes 8388608 | tf_op jit(solution)/shard_map/reshape;reshape | solution.py:72
  217.4 32.4 %fusion = (f32[512,8,4]{0,2,1:T(4,128)S(1)}, f32[8,1024,512,4]{2,1,3,0:T(8,128)}) fusion(pred[512,1024]{0,1:T(8,128)(4,1)S(1)} %broadcast_compare_fusion, bf16[512,8,4,128]{3,2,1,0:T(4,128)(2,1)} %reshape_reshape.3, bf16[1024,8,128,1]{2,1,0,3:T(8,128)(2,1)S(1)} %bitcast.84), kind=kOutput, calls=%fused_computation.2 | convolution fusion | flops 4345282560 | bytes 73990144 | tf_op jit(solution)/shard_map/bkgd,tkd->bkgt/dot_general | solution.py:74
  249.8 21.9 %fusion.2 = f32[512,8,4]{0,2,1:T(4,128)S(1)} fusion(f32[8,1024,512,4]{2,1,3,0:T(8,128)} %get-tuple-element.13, f32[512,8,4]{0,2,1:T(4,128)S(1)} %get-tuple-element.12, pred[512,1024]{0,1:T(8,128)(4,1)S(1)} %broadcast_compare_fusion), kind=kLoop, calls=%fused_computation.4 | loop fusion | flops 83869696 | bytes 67764224 | tf_op jit(solution)/shard_map/reduce_sum | solution.py:83
  271.8 0.8 copy.76
  272.6 2.3 add.44
  274.9 4.5 all-to-all-start.1
  279.4 29.9 %fusion.12 = bf16[512,8,4,128]{3,0,2,1:T(8,128)(2,1)} fusion(f32[512,8,4]{0,2,1:T(4,128)S(1)} %fusion.2, f32[8,1024,512,4]{2,1,3,0:T(8,128)} %get-tuple-element.13, f32[512,8,4]{0,2,1:T(4,128)S(1)} %get-tuple-element.12, pred[512,1024]{0,1:T(8,128)(4,1)S(1)} %broadcast_compare_fusion, bf16[1024,8,128,1]{2,1,0,3:T(8,128)(2,1)} %bitcast.83), kind=kOutput, calls=%fused_computation.14 | convolution fusion | flops 4383047680 | bytes 74055680 | tf_op jit(solution)/shard_map/bkgt,tkd->bkgd/dot_general | solution.py:84
  309.4 7.3 %copy.84 = bf16[512,8,4,128]{3,2,1,0:T(4,128)(2,1)} copy(bf16[512,8,4,128]{3,0,2,1:T(8,128)(2,1)} %fusion.12) | data formatting | bytes 8388608 | tf_op jit(solution)/shard_map/convert_element_type | solution.py:90
  316.7 7.8 %all_to_all.18 = bf16[32,16,4096]{2,1,0:T(8,128)(2,1)} reshape(bf16[512,8,4,128]{3,2,1,0:T(4,128)(2,1)} %copy.84) | data formatting | bytes 8388608 | tf_op jit(solution)/shard_map/all_to_all | solution.py:135
  324.5 0.0 all-to-all-done.1
  324.6 3.8 all_to_all.24
  328.4 12.6 %all-to-all-start.3 = ((bf16[32,16,4096]{2,1,0:T(8,128)(2,1)}), bf16[32,16,4096]{2,1,0:T(8,128)(2,1)}, u32[]{:S(2)}, u32[]{:S(2)}) async-start(bf16[32,16,4096]{2,1,0:T(8,128)(2,1)} %all_to_all.18), calls=%async_computation.3 | async-start | bytes 8388608 | tf_op jit(solution)/shard_map/all_to_all | solution.py:135
  341.0 0.1 reshape.156
  341.0 0.0 copy-done.3
  341.1 0.1 iota_compare_fusion
  341.2 0.3 fusion.45
  341.5 5.7 %fusion.44 = (f32[16,8,4]{2,1,0:T(8,128)S(1)}, f32[16,8,4,256]{3,2,1,0:T(4,128)S(1)}) fusion(bf16[16,8,4,128]{3,2,1,0:T(4,128)(2,1)S(1)} %reshape.156, pred[16,256]{1,0:T(8,128)(4,1)S(1)} %iota_compare_fusion, bf16[16,256,1024]{2,1,0:T(8,128)(2,1)} %param.13), kind=kOutput, calls=%fused_computation.54 | convolution fusion | flops 33947136 | bytes 9050112 | tf_op jit(solution)/shard_map/bkgd,btkd->bkgt/dot_general | solution.py:100
  347.2 0.4 fusion.29
  347.7 0.1 reshape.164
  347.8 0.1 copy.80
  348.0 0.1 copy.87
  348.1 0.1 copy.88
  348.2 4.7 fusion.22
  352.8 0.1 reshape.163
  353.0 0.1 copy.81
  353.0 0.1 reduce_max.31
  353.2 0.1 reduce_sum.52
  353.2 0.1 copy.78
  353.3 0.1 reshape_reshape_reshape.4
  353.5 4.6 mul.68
  358.1 9.4 %mul.69 = f32[32,16,4096]{2,1,0:T(8,128)} reshape(f32[32,16,32,128]{3,2,1,0:T(8,128)} %mul.68) | data formatting | bytes 16777216 | tf_op jit(solution)/shard_map/mul | solution.py:142
  367.5 162.5 %all-to-all-done.3 = bf16[32,16,4096]{2,1,0:T(8,128)(2,1)} async-done(((bf16[32,16,4096]{2,1,0:T(8,128)(2,1)}), bf16[32,16,4096]{2,1,0:T(8,128)(2,1)}, u32[]{:S(2)}, u32[]{:S(2)}) %all-to-all-start.3) | async-done | bytes 4194336 | tf_op jit(solution)/shard_map/all_to_all | solution.py:135
  530.0 5.7 %multiply_reduce_fusion = f32[16,4096]{1,0:T(8,128)S(1)} fusion(f32[32,16,4096]{2,1,0:T(8,128)} %mul.69, bf16[32,16,4096]{2,1,0:T(8,128)(2,1)} %all-to-all-done.3), kind=kLoop, calls=%fused_computation.15 | loop fusion | flops 6225920 | bytes 12845056 | tf_op jit(solution)/shard_map/reduce_sum | solution.py:142
  535.7 0.1 div.35
  535.9 0.1 div.38
  536.0 0.1 mul.71
  536.1 1.1 fusion.31
  (27 shorter events, 0.3 us)
Async XLA Ops:
  0.0 20.7 %copy-start.5 = (s32[2,1024]{1,0:T(2,128)S(1)}, s32[2,1024]{1,0:T(2,128)}, u32[]{:S(2)}) copy-start(s32[2,1024]{1,0:T(2,128)} %param.18) | copy-start | bytes 24580
  0.0 21.1 %copy-start = (bf16[64,16,1024]{2,1,0:T(8,128)(2,1)S(1)}, bf16[64,16,1024]{2,1,0:T(8,128)(2,1)}, u32[]{:S(2)}) copy-start(bf16[64,16,1024]{2,1,0:T(8,128)(2,1)} %param.16) | copy-start | bytes 6291460
  3.5 23.3 %copy-start.6 = (s32[512]{0:T(512)S(1)}, s32[512]{0:T(512)}, u32[]{:S(2)}) copy-start(s32[512]{0:T(512)} %param.19) | copy-start | bytes 6148
  3.5 206.1 %all-to-all-start = ((bf16[32,16,4096]{2,1,0:T(8,128)(2,1)}), bf16[32,16,4096]{2,1,0:T(8,128)(2,1)}, u32[]{:S(2)}, u32[]{:S(2)}) async-start(bf16[32,16,4096]{2,1,0:T(8,128)(2,1)} %stack.2), calls=%async_computation | async-start | bytes 8388608 | tf_op jit(solution)/shard_map/all_to_all | solution.py:69
  23.1 194.2 %copy-start.1 = (bf16[128,8,8,128]{3,2,1,0:T(8,128)(2,1)S(1)}, bf16[128,8,8,128]{3,2,1,0:T(8,128)(2,1)}, u32[]{:S(2)}) copy-start(bf16[128,8,8,128]{3,2,1,0:T(8,128)(2,1)} %copy.100) | copy-start | bytes 6291460
  274.9 49.7 %all-to-all-start.1 = ((f32[16,2,512]{2,1,0:T(2,128)}), f32[16,2,512]{2,1,0:T(2,128)S(1)}, u32[]{:S(2)}, u32[]{:S(2)}) async-start(f32[16,2,512]{2,1,0:T(2,128)} %add.44), calls=%async_computation.1 | async-start | bytes 131072 | tf_op jit(solution)/shard_map/all_to_all | solution.py:32
  316.7 24.3 %copy-start.2 = (bf16[16,4096]{1,0:T(8,128)(2,1)S(1)}, bf16[16,4096]{1,0:T(8,128)(2,1)}, u32[]{:S(2)}) copy-start(bf16[16,4096]{1,0:T(8,128)(2,1)} %param.10) | copy-start | bytes 393220
  316.7 24.3 %copy-start.3 = (bf16[16,1024]{1,0:T(8,128)(2,1)S(1)}, bf16[16,1024]{1,0:T(8,128)(2,1)}, u32[]{:S(2)}) copy-start(bf16[16,1024]{1,0:T(8,128)(2,1)} %param.11) | copy-start | bytes 98308
  316.7 24.4 %copy-start.7 = (s32[16]{0:T(128)S(1)}, s32[16]{0:T(128)}, u32[]{:S(2)}) copy-start(s32[16]{0:T(128)} %param.15) | copy-start | bytes 196
  328.4 19.6 %copy-start.4 = (bf16[16,1024]{1,0:T(8,128)(2,1)S(1)}, bf16[16,1024]{1,0:T(8,128)(2,1)}, u32[]{:S(2)}) copy-start(bf16[16,1024]{1,0:T(8,128)(2,1)} %param.12) | copy-start | bytes 98308
  328.4 201.7 %all-to-all-start.3 = ((bf16[32,16,4096]{2,1,0:T(8,128)(2,1)}), bf16[32,16,4096]{2,1,0:T(8,128)(2,1)}, u32[]{:S(2)}, u32[]{:S(2)}) async-start(bf16[32,16,4096]{2,1,0:T(8,128)(2,1)} %all_to_all.18), calls=%async_computation.3 | async-start | bytes 8388608 | tf_op jit(solution)/shard_map/all_to_all | solution.py:135
